TPU v7x, 32 devices: a whole 2x2x4 slice. The times are simulated.
32 devices in a mesh: grp: 2 (over x), shard: 16 (over z, y, core).
Axes of the slice: x: 2, y: 2, z: 4, core: 2. Of those that a mesh axis runs over, the one named last changes fastest.
Arguments:
- window: bfloat16 [32, 4096], P('grp'), may hold values from -6 to 6
- weight: bfloat16 [11008, 4096], P('shard'), may hold values from -0.09375 to 0.09375
- factor_a: bfloat16 [64, 4, 4096], P(('grp', 'shard')), may hold values from -6 to 6
- factor_b: bfloat16 [64, 4, 11008], P(('grp', 'shard')), may hold values from -6 to 6
- fitness: float32 [64], P(('grp', 'shard')), may hold values from -4 to 4
Outputs:
- perturbed: bfloat16 [11008, 1024], P('shard', 'grp')
- update: float32 [11008, 4096], P('shard', 'grp')
All inputs are finite; a program needn't handle non-finite values.
Results may differ from a plain program's by a relative error of at most 0.0029.
Values may be sent and summed in bfloat16 or wider, within the bound.
A program may use at most 64 MiB of HBM per device.

v0:
```python
import functools
import math

import jax
import jax.numpy as jnp
from jax import lax
from jax.experimental import pallas as pl
from jax.experimental.pallas import tpu as pltpu
from jax.sharding import PartitionSpec as P

MESH = pl.DeviceIdType.MESH
F32 = jnp.float32
BF16 = jnp.bfloat16
ROW_CHUNK = 128


def dot_rows(left, right):
    return lax.dot_general(left, right, (((1,), (1,)), ((), ())), preferred_element_type=F32)


def dot_cols(left, right):
    return lax.dot_general(left, right, (((0,), (0,)), ((), ())), preferred_element_type=F32)


def exchange_kernel(
    n_grp, n_shard, fit_hbm, win_hbm, a_hbm, b_hbm, weight_ref,
    a_all, b_all, small_all, base_ref,
    fit_ref, win_ref, a_ref, b_ref, in_sem,
    a_rows, b_slabs, small, weight, w_sem, b_send, b_recv, b_send_x, b_recv_x, s_send, s_recv,
    a_send, a_send_z, a_send_y, a_send_c, a_recv, a_recv_z, a_recv_y, a_recv_c,
):
    depth = n_shard // 8
    count = n_grp * n_shard
    line = n_grp * depth
    grp = lax.axis_index("grp")
    shard = lax.axis_index("shard")
    core = shard % 2
    y = (shard // 2) % 2
    low_z = (shard // 4) % 2
    high_z = shard // 8
    me = grp * n_shard + shard
    half = a_all.shape[2]
    cand_dev, rank, _ = a_ref.shape
    rows = cand_dev * rank
    ff = weight_ref.shape[0]
    tok = win_ref.shape[0]

    def slot_of(c, yy, lz, i):
        return i // depth * n_shard + ((c * 2 + yy) * 2 + lz) * depth + i % depth

    def slot_at(s):
        return slot_of(s % 2, s // 2 % 2, s // 4 % 2, grp * depth + s // 8)

    own = slot_at(shard)

    inputs = [
        pltpu.make_async_copy(src, dst, in_sem.at[i])
        for i, (src, dst) in enumerate(
            [(a_hbm, a_ref), (b_hbm, b_ref), (win_hbm, win_ref), (fit_hbm, fit_ref)]
        )
    ]
    for load in inputs:
        load.start()

    barrier = pltpu.get_barrier_semaphore()

    def greet(i, carry):
        t = (me + i) % count
        pl.semaphore_signal(
            barrier, inc=1, device_id=(t // n_shard, t % n_shard), device_id_type=MESH
        )
        return carry

    lax.fori_loop(1, count, greet, 0)

    chunks = [(lo, min(ROW_CHUNK, ff - lo)) for lo in range(0, ff, ROW_CHUNK)]
    loads = [
        pltpu.make_async_copy(
            weight_ref.at[pl.ds(lo, size)], weight.at[pl.ds(lo, size)], w_sem.at[i]
        )
        for i, (lo, size) in enumerate(chunks)
    ]
    for load in loads:
        load.start()

    inputs[0].wait()
    a_rows[...] = jnp.concatenate(
        [a_ref[j].astype(F32) for j in range(cand_dev)], axis=0
    ).astype(BF16)
    inputs[1].wait()
    for k in range(n_shard):
        b_slabs[k] = jnp.concatenate(
            [b_ref[j, :, k * ff : (k + 1) * ff].astype(F32) for j in range(cand_dev)], axis=0
        ).astype(BF16)

    pl.semaphore_wait(barrier, count - 1)

    def origin(i):
        g = (grp + n_grp - i // depth) % n_grp
        return g * depth + (high_z + depth - i % depth) % depth

    def a_source(g):
        return a_rows.at[:, pl.ds(pl.multiple_of(g * half, half), half)]

    def send_a(i, carry):
        g = (grp + i // depth) % n_grp
        h = (high_z + i) % depth
        pltpu.make_async_remote_copy(
            src_ref=a_source(g),
            dst_ref=a_all.at[own],
            send_sem=a_send,
            recv_sem=a_recv.at[i],
            device_id=(g, h * 8 + low_z * 4 + y * 2 + core),
            device_id_type=MESH,
        ).start()
        return carry

    lax.fori_loop(1, line, send_a, 0)
    pltpu.make_async_copy(a_source(grp), a_all.at[own], a_recv.at[0]).start()

    def send_b(i, carry):
        to = (shard + i) % n_shard
        pltpu.make_async_remote_copy(
            src_ref=b_slabs.at[to],
            dst_ref=b_all.at[own],
            send_sem=b_send,
            recv_sem=b_recv.at[i],
            device_id=(grp, to),
            device_id_type=MESH,
        ).start()
        return carry

    def cross_b(src, slot):
        def one(k, carry):
            pltpu.make_async_remote_copy(
                src_ref=src,
                dst_ref=b_all.at[slot],
                send_sem=b_send_x,
                recv_sem=b_recv_x,
                device_id=((grp + k) % n_grp, shard),
                device_id_type=MESH,
            ).start()
            return carry

        lax.fori_loop(1, n_grp, one, 0)

    def relay_b(i, carry):
        wait_bytes(b_all.at[0], b_recv.at[i])
        slot = slot_at((shard + n_shard - i) % n_shard)
        cross_b(b_all.at[slot], slot)
        return carry

    def forward(slot, c, yy, lz, send_sem, recv_sem):
        pltpu.make_async_remote_copy(
            src_ref=a_all.at[slot],
            dst_ref=a_all.at[slot],
            send_sem=send_sem,
            recv_sem=recv_sem,
            device_id=(grp, high_z * 8 + lz * 4 + yy * 2 + c),
            device_id_type=MESH,
        ).start()

    def wait_bytes(ref, sem):
        pltpu.make_async_copy(ref, ref, sem).wait()

    def relay(i, carry):
        wait_bytes(a_all.at[0], a_recv.at[i])
        slot = slot_of(core, y, low_z, origin(i))
        forward(slot, core, y, 1 - low_z, a_send_z, a_recv_z.at[i])
        forward(slot, core, 1 - y, low_z, a_send_y, a_recv_y.at[i])
        forward(slot, 1 - core, y, low_z, a_send_c, a_recv_c)
        return carry

    def relay_z(i, carry):
        wait_bytes(a_all.at[0], a_recv_z.at[i])
        slot = slot_of(core, y, 1 - low_z, origin(i))
        forward(slot, core, 1 - y, low_z, a_send_y, a_recv_y.at[line + i])
        forward(slot, 1 - core, y, low_z, a_send_c, a_recv_c)
        return carry

    def relay_y(i, carry):
        wait_bytes(a_all.at[0], a_recv_y.at[i])
        lz = (low_z + i // line) % 2
        slot = slot_of(core, 1 - y, lz, origin(i % line))
        forward(slot, 1 - core, y, low_z, a_send_c, a_recv_c)
        return carry

    lax.fori_loop(0, 1, relay, 0)
    cross_b(b_slabs.at[shard], own)
    pltpu.make_async_copy(b_slabs.at[shard], b_all.at[own], b_recv.at[0]).start()
    lax.fori_loop(1, n_shard, send_b, 0)

    inputs[2].wait()
    inputs[3].wait()
    wide = rows * tok
    win = jnp.concatenate([win_ref[...]] * rows, axis=0)
    projected = dot_rows(a_rows[...], win)
    lane = lax.broadcasted_iota(jnp.int32, (rows, wide), 1)
    row = lax.broadcasted_iota(jnp.int32, (rows, wide), 0)
    small[0:1, :] = jnp.sum(jnp.where(lane // tok == row, projected, 0.0), axis=0, keepdims=True)
    lane = lax.broadcasted_iota(jnp.int32, (1, wide), 1)
    fit = jnp.zeros((1, wide), F32)
    for j in range(cand_dev):
        fit = jnp.where(lane // rank == j, fit_ref[j], fit)
    small[1:2, :] = fit

    def base_chunk(i):
        lo, size = chunks[i]
        loads[i].wait()
        base = dot_rows(weight[pl.ds(lo, size)], win)
        high = base.astype(BF16)
        rest = base - high.astype(F32)
        mid = rest.astype(BF16)
        low = rest - mid.astype(F32)
        part = lax.broadcasted_iota(jnp.int32, base.shape, 1) // tok
        terms = jnp.where(part == 0, high.astype(F32), jnp.where(part == 1, mid.astype(F32), low))
        base_ref[pl.ds(lo, size), :] = jnp.where(part < 3, terms, 0.0).astype(BF16)

    def send_small(i, carry):
        t = (me + i) % count
        pltpu.make_async_remote_copy(
            src_ref=small,
            dst_ref=small_all.at[own],
            send_sem=s_send,
            recv_sem=s_recv,
            device_id=(t // n_shard, t % n_shard),
            device_id_type=MESH,
        ).start()
        return carry

    lax.fori_loop(1, line, relay, 0)
    for i in range(0, 1):
        base_chunk(i)
    lax.fori_loop(1, n_shard // 2, relay_b, 0)
    lax.fori_loop(0, line, relay_z, 0)
    lax.fori_loop(1, count, send_small, 0)
    pltpu.make_async_copy(small, small_all.at[own], s_recv).start()
    lax.fori_loop(n_shard // 2, n_shard, relay_b, 0)
    for i in range(1, len(chunks)):
        base_chunk(i)
    lax.fori_loop(0, 2 * line, relay_y, 0)

    wait_bytes(small_all, s_recv)
    wait_bytes(b_all.at[0], b_recv.at[0])
    wait_bytes(b_all.at[pl.ds(0, count - n_shard)], b_recv_x)
    wait_bytes(b_all.at[pl.ds(0, count - n_shard)], b_send_x)
    wait_bytes(a_all.at[pl.ds(0, 4 * line)], a_recv_c)
    wait_bytes(a_all.at[pl.ds(0, line - 1)], a_send)
    wait_bytes(a_all.at[pl.ds(0, line)], a_send_z)
    wait_bytes(a_all.at[pl.ds(0, 2 * line)], a_send_y)
    wait_bytes(a_all.at[pl.ds(0, 4 * line)], a_send_c)
    wait_bytes(b_all.at[pl.ds(0, n_shard - 1)], b_send)
    wait_bytes(small_all.at[pl.ds(0, count - 1)], s_send)


def combine_kernel(
    n_grp, n_shard, tok, rank, perturb, step_scale,
    a_ref, b_ref, small_ref, base_ref, pert_ref, upd_ref, weighted,
):
    depth = n_shard // 8
    count, rows, ff = b_ref.shape
    wide = small_ref.shape[2]
    step = pl.program_id(0)
    cand_dev = rows // rank

    @pl.when(step == 0)
    def _():
        shape = (count, rows, wide)
        pick = lax.broadcasted_iota(jnp.int32, shape, 2) == lax.broadcasted_iota(jnp.int32, shape, 1)
        fit = jnp.broadcast_to(small_ref[:, 1:2, :], shape)
        fit = jnp.sum(jnp.where(pick, fit, 0.0), axis=2, keepdims=True)
        scaled = fit * b_ref[...].astype(F32)
        weighted[...] = scaled.reshape(count * rows, ff).astype(BF16)

    width = upd_ref.shape[1]
    at = pl.ds(pl.multiple_of(step * width, width), width)
    block = a_ref[:, :, at].astype(F32).reshape(count * rows, width).astype(BF16)
    upd_ref[...] = dot_cols(weighted[...], block) * step_scale

    @pl.when(step == 0)
    def _():
        grp = lax.axis_index("grp")
        cols = pert_ref.shape[1]
        mine = pl.ds(grp * n_shard, n_shard)
        k = n_shard * rows
        shape = (n_shard, rows, wide)
        keep = (
            lax.broadcasted_iota(jnp.int32, shape, 2) // tok
            == lax.broadcasted_iota(jnp.int32, shape, 1)
        )
        own_b = b_ref[mine].astype(F32)
        own_p = jnp.broadcast_to(small_ref[mine, 0:1, :], shape) * perturb
        own_p = jnp.where(keep, own_p, 0.0)
        own_b = own_b.reshape(k, ff).astype(BF16)
        own_p = own_p.reshape(k, wide)
        high = own_p.astype(BF16)
        low = (own_p - high.astype(F32)).astype(BF16)
        spread = (
            lax.broadcasted_iota(jnp.int32, (wide, cols), 1) % tok
            == lax.broadcasted_iota(jnp.int32, (wide, cols), 0) % tok
        ).astype(F32).astype(BF16)
        r = lax.broadcasted_iota(jnp.int32, (k, cols), 0)
        slab = r // rows
        cyz = slab // depth
        sh = (slab % depth) * 8 + (cyz % 2) * 4 + (cyz // 2 % 2) * 2 + cyz // 4
        cand = sh * cand_dev + (r % rows) // rank
        same = cand == lax.broadcasted_iota(jnp.int32, (k, cols), 1) // tok

        def blocks(v):
            return jnp.where(same, jnp.dot(v, spread, preferred_element_type=F32), 0.0).astype(BF16)

        total = jnp.dot(base_ref[...], spread, preferred_element_type=F32)
        total = total + dot_cols(own_b, blocks(high)) + dot_cols(own_b, blocks(low))
        pert_ref[...] = total.astype(BF16)


def local(window, weight, factor_a, factor_b, fitness):
    tok, model_width = window.shape
    cand_dev, rank, _ = factor_a.shape
    n_shard = lax.axis_size("shard")
    n_grp = lax.axis_size("grp")
    total_cands = cand_dev * n_grp * n_shard
    perturb = 0.25 / math.sqrt(model_width)
    step_scale = 0.5 / math.sqrt(total_cands)
    rows = cand_dev * rank
    ff = weight.shape[0]
    half = model_width // n_grp
    count = n_grp * n_shard
    line = n_grp * (n_shard // 8)
    wide = rows * tok

    operands = (fitness, window, factor_a, factor_b, weight)
    n_chunks = -(-ff // ROW_CHUNK)
    vmem = pl.BlockSpec(memory_space=pltpu.VMEM)
    dma = pltpu.SemaphoreType.DMA
    a_all, b_all, small_all, base = pl.pallas_call(
        functools.partial(exchange_kernel, n_grp, n_shard),
        out_shape=(
            jax.ShapeDtypeStruct((count, rows, half), BF16),
            jax.ShapeDtypeStruct((count, rows, ff), BF16),
            jax.ShapeDtypeStruct((count, 2, wide), F32),
            jax.ShapeDtypeStruct((ff, wide), BF16),
        ),
        in_specs=[pl.BlockSpec(memory_space=pltpu.HBM)] * 5,
        out_specs=(vmem, vmem, vmem, vmem),
        scratch_shapes=[
            pltpu.SMEM(fitness.shape, F32),
            pltpu.VMEM(window.shape, BF16),
            pltpu.VMEM(factor_a.shape, BF16),
            pltpu.VMEM(factor_b.shape, BF16),
            dma((4,)),
            pltpu.VMEM((rows, model_width), BF16),
            pltpu.VMEM((n_shard, rows, ff), BF16),
            pltpu.VMEM((2, wide), F32),
            pltpu.VMEM((ff, model_width), BF16),
            dma((n_chunks,)),
            dma, dma((n_shard,)), dma, dma, dma, dma, dma, dma, dma, dma,
            dma((line,)), dma((line,)), dma((2 * line,)), dma,
        ],
        compiler_params=pltpu.CompilerParams(
            collective_id=0, has_side_effects=True, vmem_limit_bytes=50 * 1024 * 1024
        ),
        name="exchange",
    )(*[pltpu.with_memory_space_constraint(v, pltpu.HBM) for v in operands])

    block = min(half, 1024)
    cols = n_shard * cand_dev * tok
    whole = lambda shape: pl.BlockSpec(shape, lambda i: (0,) * len(shape))
    perturbed, update = pl.pallas_call(
        functools.partial(combine_kernel, n_grp, n_shard, tok, rank, perturb, step_scale),
        out_shape=(
            jax.ShapeDtypeStruct((ff, cols), BF16),
            jax.ShapeDtypeStruct((ff, half), F32),
        ),
        grid=(half // block,),
        in_specs=[
            vmem, vmem, vmem, vmem,
        ],
        out_specs=(
            whole((ff, cols)),
            pl.BlockSpec((ff, block), lambda i: (0, i)),
        ),
        scratch_shapes=[pltpu.VMEM((count * rows, ff), BF16)],
        compiler_params=pltpu.CompilerParams(vmem_limit_bytes=40 * 1024 * 1024),
        name="combine",
    )(a_all, b_all, small_all, base)
    return perturbed, update


def solution(mesh):
    in_specs = (
        P("grp", None),
        P("shard", None),
        P(("grp", "shard"), None, None),
        P(("grp", "shard"), None, None),
        P(("grp", "shard")),
    )
    out_specs = (P("shard", "grp"), P("shard", "grp"))
    return jax.shard_map(local, mesh=mesh, in_specs=in_specs, out_specs=out_specs, check_vma=False)
```

profile of v0, /device:TPU:0, one launch (start us, length us, event | category | flops | bytes accessed | tf_op | source)
XLA Modules:
  0.0 27.0 jit_solution(5628582341943467212)
XLA Ops:
  0.6 21.9 %exchange.1 = (bf16[32,8,2048]{2,1,0:T(8,128)(2,1)S(1)}, bf16[32,8,688]{2,1,0:T(8,128)(2,1)S(1)}, f32[32,2,128]{2,1,0:T(2,128)S(1)}, bf16[688,128]{1,0:T(8,128)(2,1)S(1)}) custom-call(f32[2]{0:T(128)} %fit_hbm.1, bf16[16,4096]{1,0:T(8,128)(2,1)} %win_hbm.1, bf16[2,4,4096]{2,1,0:T(4,128)(2,1)} %a_hbm.1, bf16[2,4,11008]{2,1,0:T(4,128)(2,1)} %b_hbm.1, ...), custom_call_target="tpu_custom_call" | custom-call | tf_op jit(solution)/shard_map/exchange/pallas_call | solution.py:336
  22.5 4.5 %combine.1 = (bf16[688,512]{1,0:T(8,128)(2,1)}, f32[688,2048]{1,0:T(8,128)}) custom-call(bf16[32,8,2048]{2,1,0:T(8,128)(2,1)S(1)} %get-tuple-element.6.a_ref, bf16[32,8,688]{2,1,0:T(8,128)(2,1)S(1)} %get-tuple-element.7.b_ref, f32[32,2,128]{2,1,0:T(2,128)S(1)} %get-tuple-element.8.small_ref, bf16[688,128]{1,0:T(8,128)(2,1)S(1)} %get-tuple-element.9.base_ref), custom_call_target="tpu_custom_call" | custom-call | tf_op jit(solution)/shard_map/combine/pallas_call | solution.py:369
where the time goes:
time: 27.1 us; the launch traced here: 27 us
  Pallas kernels  26.4 us (97%)
  between operations  0.64 us (2%)
    pallas_call x1, Pallas kernels, local(): pl.pallas_call(functools.partial(exchange_kernel, n_grp, n_shard), out_sh...  21.9 us
    pallas_call x1, Pallas kernels, local(): pl.pallas_call(functools.partial(combine_kernel, n_grp, n_shard, tok, ran...  4.46 us

commit v1 on v0

v1 whole, which is shorter than its diff:
```python
import functools
import math

import jax
import jax.numpy as jnp
from jax import lax
from jax.experimental import pallas as pl
from jax.experimental.pallas import tpu as pltpu
from jax.sharding import PartitionSpec as P

MESH = pl.DeviceIdType.MESH
F32 = jnp.float32
BF16 = jnp.bfloat16
ROW_CHUNK = 256
COL_BLOCK = 512


def dot_rows(left, right):
    return lax.dot_general(left, right, (((1,), (1,)), ((), ())), preferred_element_type=F32)


def dot_cols(left, right):
    return lax.dot_general(left, right, (((0,), (0,)), ((), ())), preferred_element_type=F32)


def split3(v):
    high = v.astype(BF16)
    rest = v - high.astype(F32)
    mid = rest.astype(BF16)
    low = (rest - mid.astype(F32)).astype(BF16)
    return high, mid, low


def exchange_kernel(
    n_grp, n_shard, perturb, fit_hbm, win_hbm, a_hbm, b_hbm, weight_ref,
    a_all, weighted, pert_ref,
    fit_ref, win_ref, a_ref, b_ref, in_sem,
    a_rows, b_slabs, b_all, weight, w_sem, b_send, b_recv, b_send_x, b_recv_x,
    a_send, a_send_z, a_send_y, a_send_c, a_recv, a_recv_z, a_recv_y, a_recv_c,
):
    depth = n_shard // 8
    count = n_grp * n_shard
    line = n_grp * depth
    grp = lax.axis_index("grp")
    shard = lax.axis_index("shard")
    core = shard % 2
    y = (shard // 2) % 2
    low_z = (shard // 4) % 2
    high_z = shard // 8
    half = a_all.shape[2]
    cand_dev, rank, _ = a_ref.shape
    rows = cand_dev * rank
    ff = weight_ref.shape[0]
    tok = win_ref.shape[0]
    wide = b_all.shape[2]
    cols = pert_ref.shape[1]

    def slot_of(c, yy, lz, i):
        return i // depth * n_shard + ((c * 2 + yy) * 2 + lz) * depth + i % depth

    def slot_at(s):
        return slot_of(s % 2, s // 2 % 2, s // 4 % 2, grp * depth + s // 8)

    own = slot_at(shard)

    inputs = [
        pltpu.make_async_copy(src, dst, in_sem.at[i])
        for i, (src, dst) in enumerate(
            [(a_hbm, a_ref), (b_hbm, b_ref), (win_hbm, win_ref), (fit_hbm, fit_ref)]
        )
    ]
    for load in inputs:
        load.start()

    barrier = pltpu.get_barrier_semaphore()

    def line_peer(i):
        return ((grp + i // depth) % n_grp, (high_z + i) % depth * 8 + low_z * 4 + y * 2 + core)

    def greet_shard(i, carry):
        pl.semaphore_signal(
            barrier, inc=1, device_id=(grp, (shard + i) % n_shard), device_id_type=MESH
        )
        return carry

    def greet_line(i, carry):
        pl.semaphore_signal(barrier, inc=1, device_id=line_peer(i), device_id_type=MESH)
        return carry

    lax.fori_loop(1, n_shard, greet_shard, 0)
    lax.fori_loop(depth, line, greet_line, 0)

    chunks = [(lo, min(ROW_CHUNK, ff - lo)) for lo in range(0, ff, ROW_CHUNK)]
    loads = [
        pltpu.make_async_copy(
            weight_ref.at[pl.ds(lo, size)], weight.at[pl.ds(lo, size)], w_sem.at[i]
        )
        for i, (lo, size) in enumerate(chunks)
    ]
    for load in loads:
        load.start()

    inputs[0].wait()
    a_rows[...] = jnp.concatenate(
        [a_ref[j].astype(F32) for j in range(cand_dev)], axis=0
    ).astype(BF16)

    pl.semaphore_wait(barrier, n_shard - 1 + line - depth)

    def origin(i):
        g = (grp + n_grp - i // depth) % n_grp
        return g * depth + (high_z + depth - i % depth) % depth

    def a_source(g):
        return a_rows.at[:, pl.ds(pl.multiple_of(g * half, half), half)]

    def send_a(i, carry):
        pltpu.make_async_remote_copy(
            src_ref=a_source((grp + i // depth) % n_grp),
            dst_ref=a_all.at[own],
            send_sem=a_send,
            recv_sem=a_recv.at[i],
            device_id=line_peer(i),
            device_id_type=MESH,
        ).start()
        return carry

    def send_b(i, carry):
        to = (shard + i) % n_shard
        pltpu.make_async_remote_copy(
            src_ref=b_slabs.at[to],
            dst_ref=b_all.at[own],
            send_sem=b_send,
            recv_sem=b_recv.at[i],
            device_id=(grp, to),
            device_id_type=MESH,
        ).start()
        return carry

    def cross_b(src, slot):
        def one(k, carry):
            pltpu.make_async_remote_copy(
                src_ref=src,
                dst_ref=b_all.at[slot],
                send_sem=b_send_x,
                recv_sem=b_recv_x,
                device_id=((grp + k) % n_grp, shard),
                device_id_type=MESH,
            ).start()
            return carry

        lax.fori_loop(1, n_grp, one, 0)

    def wait_bytes(ref, sem):
        pltpu.make_async_copy(ref, ref, sem).wait()

    def relay_b(i, carry):
        wait_bytes(b_all.at[0], b_recv.at[i])
        slot = slot_at((shard + n_shard - i) % n_shard)
        cross_b(b_all.at[slot], slot)
        return carry

    def forward(src, slot, c, yy, lz, send_sem, recv_sem):
        pltpu.make_async_remote_copy(
            src_ref=src,
            dst_ref=a_all.at[slot],
            send_sem=send_sem,
            recv_sem=recv_sem,
            device_id=(grp, high_z * 8 + lz * 4 + yy * 2 + c),
            device_id_type=MESH,
        ).start()

    def spread_a(src, slot, i):
        forward(src, slot, core, y, 1 - low_z, a_send_z, a_recv_z.at[i])
        forward(src, slot, core, 1 - y, low_z, a_send_y, a_recv_y.at[i])
        forward(src, slot, 1 - core, y, low_z, a_send_c, a_recv_c)

    def relay(i, carry):
        wait_bytes(a_all.at[0], a_recv.at[i])
        slot = slot_of(core, y, low_z, origin(i))
        spread_a(a_all.at[slot], slot, i)
        return carry

    def relay_z(i, carry):
        wait_bytes(a_all.at[0], a_recv_z.at[i])
        slot = slot_of(core, y, 1 - low_z, origin(i))
        forward(a_all.at[slot], slot, core, 1 - y, low_z, a_send_y, a_recv_y.at[line + i])
        forward(a_all.at[slot], slot, 1 - core, y, low_z, a_send_c, a_recv_c)
        return carry

    def relay_y(i, carry):
        wait_bytes(a_all.at[0], a_recv_y.at[i])
        lz = (low_z + i // line) % 2
        slot = slot_of(core, 1 - y, lz, origin(i % line))
        forward(a_all.at[slot], slot, 1 - core, y, low_z, a_send_c, a_recv_c)
        return carry

    lax.fori_loop(1, line, send_a, 0)
    spread_a(a_source(grp), own, 0)

    for load in inputs[1:]:
        load.wait()
    projected = dot_rows(a_rows[...], win_ref[...]) * perturb
    high = projected.astype(BF16)
    low = (projected - high.astype(F32)).astype(BF16)
    row = lax.broadcasted_iota(jnp.int32, (rows, 1), 0)
    fit = jnp.zeros((rows, 1), F32)
    for j in range(cand_dev):
        fit = jnp.where(row // rank == j, fit_ref[j], fit)
    extra = [high, low, *split3(fit)]
    extra.append(jnp.zeros((rows, wide - ff - sum(v.shape[1] for v in extra)), BF16))
    extra = jnp.concatenate([v.astype(F32) for v in extra], axis=1)
    for k in range(n_shard):
        slab = jnp.concatenate(
            [b_ref[j, :, k * ff : (k + 1) * ff].astype(F32) for j in range(cand_dev)], axis=0
        )
        b_slabs[k] = jnp.concatenate([slab, extra], axis=1).astype(BF16)

    lax.fori_loop(1, n_shard, send_b, 0)
    cross_b(b_slabs.at[shard], own)
    b_all[own] = b_slabs[shard]
    a_all[own] = a_rows[:, pl.ds(pl.multiple_of(grp * half, half), half)]

    parts = []
    for (lo, size), load in zip(chunks, loads):
        load.wait()
        parts.append(dot_rows(win_ref[...], weight[pl.ds(lo, size)]))
    base = jnp.concatenate(split3(jnp.concatenate(parts, axis=1)), axis=0)

    def relay_far(j, carry):
        return relay(j // (depth - 1) * depth + j % (depth - 1) + 1, carry)

    lax.fori_loop(0, 1, relay_z, 0)
    lax.fori_loop(0, 1, relay_y, 0)
    lax.fori_loop(1, n_grp, lambda k, carry: relay(k * depth, carry), 0)
    if depth > 1:
        lax.fori_loop(0, n_grp * (depth - 1), relay_far, 0)
    lax.fori_loop(1, n_shard // 2, relay_b, 0)
    lax.fori_loop(1, line, relay_z, 0)
    lax.fori_loop(n_shard // 2, n_shard, relay_b, 0)
    lax.fori_loop(1, 2 * line, relay_y, 0)

    wait_bytes(b_all.at[pl.ds(0, count - n_shard)], b_recv_x)

    lane = lax.broadcasted_iota(jnp.int32, (count, rows, wide - ff), 2)
    every = b_all[:, :, ff:].astype(F32)
    scale = jnp.sum(
        jnp.where((lane >= 2 * tok) & (lane < 2 * tok + 3), every, 0.0), axis=2, keepdims=True
    )
    scaled = b_all[:, :, :ff].astype(F32) * scale
    weighted[...] = scaled.reshape(count * rows, ff).astype(BF16)

    mine = pl.ds(grp * n_shard, n_shard)
    k = n_shard * rows
    own_b = b_all[mine, :, :ff].astype(F32).reshape(k, ff).astype(BF16)
    start = ff // 128 * 128
    codes = b_all[mine, :, start:].astype(F32).reshape(k, wide - start).astype(BF16)
    r = lax.broadcasted_iota(jnp.int32, (k, cols), 0)
    slab = r // rows
    cyz = slab // depth
    sh = (slab % depth) * 8 + (cyz % 2) * 4 + (cyz // 2 % 2) * 2 + cyz // 4
    cand = sh * cand_dev + (r % rows) // rank
    same = cand == lax.broadcasted_iota(jnp.int32, (k, cols), 1) // tok

    def pick(depth_in, first):
        at = lax.broadcasted_iota(jnp.int32, (depth_in, cols), 0) - first
        to = lax.broadcasted_iota(jnp.int32, (depth_in, cols), 1) % tok
        return at, to

    def blocks(first):
        at, to = pick(wide - start, ff - start + first)
        chosen = (at == to).astype(F32).astype(BF16)
        spread = jnp.dot(codes, chosen, preferred_element_type=F32)
        return jnp.where(same, spread, 0.0).astype(BF16)

    at, to = pick(3 * tok, 0)
    total = dot_cols(base, (at % tok == to).astype(F32).astype(BF16))
    total = total + dot_cols(own_b, blocks(0)) + dot_cols(own_b, blocks(tok))
    pert_ref[...] = total.astype(BF16)

    wait_bytes(a_all.at[pl.ds(0, 4 * line)], a_recv_c)
    wait_bytes(b_all.at[pl.ds(0, count - n_shard)], b_send_x)
    wait_bytes(a_all.at[pl.ds(0, line - 1)], a_send)
    wait_bytes(a_all.at[pl.ds(0, line)], a_send_z)
    wait_bytes(a_all.at[pl.ds(0, 2 * line)], a_send_y)
    wait_bytes(a_all.at[pl.ds(0, 4 * line)], a_send_c)
    wait_bytes(b_all.at[pl.ds(0, n_shard - 1)], b_send)


def combine_kernel(step_scale, a_ref, weighted, pert_ref, pert_out, upd_out, upd, p_sem, u_sem):
    count, rows, half = a_ref.shape
    store = pltpu.make_async_copy(pert_ref, pert_out, p_sem)
    store.start()
    stores = []
    for n, lo in enumerate(range(0, half, COL_BLOCK)):
        at = pl.ds(lo, min(COL_BLOCK, half - lo))
        block = a_ref[:, :, at].reshape(count * rows, at.size)
        upd[:, at] = dot_cols(weighted[...], block) * step_scale
        stores.append(pltpu.make_async_copy(upd.at[:, at], upd_out.at[:, at], u_sem.at[n]))
        stores[-1].start()
    store.wait()
    for done in stores:
        done.wait()


def local(window, weight, factor_a, factor_b, fitness):
    tok, model_width = window.shape
    cand_dev, rank, _ = factor_a.shape
    n_shard = lax.axis_size("shard")
    n_grp = lax.axis_size("grp")
    total_cands = cand_dev * n_grp * n_shard
    perturb = 0.25 / math.sqrt(model_width)
    step_scale = 0.5 / math.sqrt(total_cands)
    rows = cand_dev * rank
    ff = weight.shape[0]
    half = model_width // n_grp
    count = n_grp * n_shard
    line = n_grp * (n_shard // 8)
    wide = -(-(ff + 2 * tok + 3) // 128) * 128
    cols = n_shard * cand_dev * tok

    operands = (fitness, window, factor_a, factor_b, weight)
    n_chunks = -(-ff // ROW_CHUNK)
    vmem = pl.BlockSpec(memory_space=pltpu.VMEM)
    hbm = pl.BlockSpec(memory_space=pltpu.HBM)
    dma = pltpu.SemaphoreType.DMA
    a_all, weighted, pert = pl.pallas_call(
        functools.partial(exchange_kernel, n_grp, n_shard, perturb),
        out_shape=(
            jax.ShapeDtypeStruct((count, rows, half), BF16),
            jax.ShapeDtypeStruct((count * rows, ff), BF16),
            jax.ShapeDtypeStruct((ff, cols), BF16),
        ),
        in_specs=[hbm] * 5,
        out_specs=(vmem, vmem, vmem),
        scratch_shapes=[
            pltpu.SMEM(fitness.shape, F32),
            pltpu.VMEM(window.shape, BF16),
            pltpu.VMEM(factor_a.shape, BF16),
            pltpu.VMEM(factor_b.shape, BF16),
            dma((4,)),
            pltpu.VMEM((rows, model_width), BF16),
            pltpu.VMEM((n_shard, rows, wide), BF16),
            pltpu.VMEM((count, rows, wide), BF16),
            pltpu.VMEM((ff, model_width), BF16),
            dma((n_chunks,)),
            dma, dma((n_shard,)), dma, dma, dma, dma, dma, dma,
            dma((line,)), dma((line,)), dma((2 * line,)), dma,
        ],
        compiler_params=pltpu.CompilerParams(
            collective_id=0, has_side_effects=True, vmem_limit_bytes=50 * 1024 * 1024
        ),
        name="exchange",
    )(*[pltpu.with_memory_space_constraint(v, pltpu.HBM) for v in operands])

    perturbed, update = pl.pallas_call(
        functools.partial(combine_kernel, step_scale),
        out_shape=(
            jax.ShapeDtypeStruct((ff, cols), BF16),
            jax.ShapeDtypeStruct((ff, half), F32),
        ),
        in_specs=[vmem, vmem, vmem],
        out_specs=(hbm, hbm),
        scratch_shapes=[pltpu.VMEM((ff, half), F32), dma, dma((-(-half // COL_BLOCK),))],
        compiler_params=pltpu.CompilerParams(vmem_limit_bytes=40 * 1024 * 1024),
        name="combine",
    )(a_all, weighted, pert)
    return perturbed, update


def solution(mesh):
    in_specs = (
        P("grp", None),
        P("shard", None),
        P(("grp", "shard"), None, None),
        P(("grp", "shard"), None, None),
        P(("grp", "shard")),
    )
    out_specs = (P("shard", "grp"), P("shard", "grp"))
    return jax.shard_map(local, mesh=mesh, in_specs=in_specs, out_specs=out_specs, check_vma=False)
```

time: 27.1 us -> 24.8 us (0.915)
  Pallas kernels: 26.4 us -> 24 us
    pallas_call x2, Pallas kernels: 26.4 us -> 24 us  [the longest x1 21.1 us: local(): pl.pallas_call(functools.partial(exchange_kernel, n_grp, n_shard, perturb...]
where the time goes in v1:
time: 24.8 us; the launch traced here: 24.6 us
  Pallas kernels  24 us (97%)
  between operations  0.64 us (3%)
    pallas_call x1, Pallas kernels, local(): pl.pallas_call(functools.partial(exchange_kernel, n_grp, n_shard, perturb...  21.1 us
    pallas_call x1, Pallas kernels, local(): pl.pallas_call(functools.partial(combine_kernel, step_scale), out_shape=(...  2.9 us

profile of v1, /device:TPU:0, one launch (start us, length us, event | category | flops | bytes accessed | tf_op | source)
XLA Modules:
  0.0 24.6 jit_solution(1161749882672691830)
XLA Ops:
  0.6 21.1 %exchange.1 = (bf16[32,8,2048]{2,1,0:T(8,128)(2,1)S(1)}, bf16[256,688]{1,0:T(8,128)(2,1)S(1)}, bf16[688,512]{1,0:T(8,128)(2,1)S(1)}) custom-call(f32[2]{0:T(128)} %fit_hbm.1, bf16[16,4096]{1,0:T(8,128)(2,1)} %win_hbm.1, bf16[2,4,4096]{2,1,0:T(4,128)(2,1)} %a_hbm.1, bf16[2,4,11008]{2,1,0:T(4,128)(2,1)} %b_hbm.1, bf16[688,4096]{1,0:T(8,128)(2,1)} %weight_ref.1), custom_call_target="tpu_custom_call" | custom-call | tf_op jit(solution)/shard_map/exchange/pallas_call | solution.py:327
  21.7 2.9 %combine.1 = (bf16[688,512]{1,0:T(8,128)(2,1)}, f32[688,2048]{1,0:T(8,128)}) custom-call(bf16[32,8,2048]{2,1,0:T(8,128)(2,1)S(1)} %get-tuple-element.5.a_ref, bf16[256,688]{1,0:T(8,128)(2,1)S(1)} %get-tuple-element.6.weighted, bf16[688,512]{1,0:T(8,128)(2,1)S(1)} %get-tuple-element.7.pert_ref), custom_call_target="tpu_custom_call" | custom-call | tf_op jit(solution)/shard_map/combine/pallas_call | solution.py:356
